TPU v7x, 32 devices: a whole 2x2x4 slice. The times are simulated.
32 devices in a mesh: rep: 1, r: 4 (over z), s: 8 (over x, y, core).
Axes of the slice: x: 2, y: 2, z: 4, core: 2. Of those that a mesh axis runs over, the one named last changes fastest.
Arguments:
- x: bfloat16 [32, 4096, 768], P(('rep', 'r', 's'))
- dy: bfloat16 [32, 4096, 768], P(('rep', 'r', 's'))
- w_gate: bfloat16 [2, 768, 2304], P(None, 's')
- w_up: bfloat16 [2, 768, 2304], P(None, 's')
- w_down: bfloat16 [2, 2304, 768], P(None, 's')
Outputs:
- output 1: bfloat16 [32, 4096, 768], P(('rep', 'r', 's'))
- output 2: bfloat16 [2, 768, 2304], P('rep', 's')
- output 3: bfloat16 [2, 768, 2304], P('rep', 's')
- output 4: bfloat16 [2, 2304, 768], P('rep', 's')
All inputs are finite; a program needn't handle non-finite values.
Results may differ from a plain program's by a relative error of at most 0.018.
Values are sent between devices in bfloat16 or wider.
A program may use at most 2 GiB of HBM per device.

v0:
```python
import jax
import jax.numpy as jnp
from jax import lax
from jax.sharding import PartitionSpec as P

NAMES = ("w_gate", "w_up", "w_down")


def matmul(a, w):
    return jnp.dot(a, w, preferred_element_type=jnp.float32).astype(jnp.bfloat16)


def normed(h):
    wide = h.astype(jnp.float32)
    scale = lax.rsqrt(jnp.mean(wide**2, -1, keepdims=True) + 1e-6)
    return (wide * scale).astype(jnp.bfloat16)


def layer(h, w):
    a = normed(h)
    gate = jnp.dot(a, w["w_gate"], preferred_element_type=jnp.float32)
    up = jnp.dot(a, w["w_up"], preferred_element_type=jnp.float32)
    return h + matmul((jax.nn.silu(gate) * up).astype(jnp.bfloat16), w["w_down"])


def solution(mesh):
    def fetched(weights, number):
        return {name: lax.all_gather(w[number], "s", axis=0, tiled=True) for name, w in zip(NAMES, weights, strict=True)}

    def summed(term):
        return lax.psum(lax.psum_scatter(term, "s", scatter_dimension=0, tiled=True), "r")

    def step(x, dy, *weights):
        layers = weights[0].shape[0]
        h, inputs = x[0], []
        for number in range(layers):
            inputs.append(h)
            h = layer(h, fetched(weights, number))
        by_h, mine = dy[0], [None] * layers
        for number in reversed(range(layers)):
            _, back = jax.vjp(lambda w, h: layer(h, w), fetched(weights, number), inputs[number])
            by_w, by_h = back(by_h)
            mine[number] = [summed(by_w[name]) for name in NAMES]
        return (by_h[None], *(jnp.stack([mine[number][i] for number in range(layers)]) for i in range(3)))

    states, cut = P(("rep", "r", "s"), None, None), P(None, "s", None)
    return jax.shard_map(
        step,
        mesh=mesh,
        in_specs=(states, states) + (cut,) * 3,
        out_specs=(states,) + (P("rep", "s", None),) * 3,
        check_vma=False,
    )
```

profile of v0, /device:TPU:0, one launch (start us, length us, event | category | flops | bytes accessed | tf_op | source)
XLA Modules:
  0.0 784.4 jit_solution(3587473781492497861)
XLA Ops:
  15.5 8.6 %copy.10 = bf16[1,4096,768]{1,2,0:T(8,128)(2,1)} copy(bf16[1,4096,768]{2,1,0:T(8,128)(2,1)} %param.5) | data formatting | bytes 12582912 | tf_op args[0]
  24.2 4.1 fusion.15
  28.9 8.6 %copy.9 = bf16[1,4096,768]{1,2,0:T(8,128)(2,1)} copy(bf16[1,4096,768]{2,1,0:T(8,128)(2,1)} %param.6) | data formatting | bytes 12582912 | tf_op args[1]
  37.4 9.3 %all-gather.13.cloned.1.call-done = bf16[1,768,2304]{2,1,0:T(8,128)(2,1)} async-done(((bf16[1,96,2304]{2,1,0:T(8,128)(2,1)}), bf16[1,768,2304]{2,1,0:T(8,128)(2,1)}) %all-gather.13.cloned.1.call-update) | async-done | bytes 3538960 | tf_op jit(solution)/shard_map/all_gather | solution.py:28
  46.8 23.7 %fusion.45 = f32[4096,2304]{1,0:T(8,128)} fusion(bf16[1,4096,768]{1,2,0:T(8,128)(2,1)} %copy.10, f32[4096]{0:T(1024)S(1)} %fusion.58, bf16[1,768,2304]{2,1,0:T(8,128)(2,1)} %all-gather.13.cloned.1.call-done), kind=kOutput, calls=%fused_computation.65 | convolution fusion | flops 14504951808 | bytes 47595520 | tf_op jit(solution)/shard_map/dot_general | solution.py:21
  70.5 11.8 %all-gather.15.cloned.1.call-done = bf16[1,768,2304]{2,1,0:T(8,128)(2,1)} async-done(((bf16[1,96,2304]{2,1,0:T(8,128)(2,1)}), bf16[1,768,2304]{2,1,0:T(8,128)(2,1)}) %all-gather.15.cloned.1.call-update) | async-done | bytes 3538960 | tf_op jit(solution)/shard_map/all_gather | solution.py:28
  82.3 37.9 %multiply_convert_fusion.1 = (bf16[4096,2304]{1,0:T(8,128)(2,1)}, f32[4096,2304]{1,0:T(8,128)}) fusion(f32[4096,2304]{1,0:T(8,128)} %fusion.45, bf16[1,768,2304]{2,1,0:T(8,128)(2,1)} %all-gather.15.cloned.1.call-done, bf16[1,4096,768]{1,2,0:T(8,128)(2,1)} %copy.10, f32[4096]{0:T(1024)S(1)} %fusion.58), kind=kOutput, calls=%fused_computation.13 | convolution fusion | flops 14561574912 | bytes 104218624 | tf_op jit(solution)/shard_map/dot_general | solution.py:22
  120.2 23.8 %fusion.18 = (f32[4096]{0:T(1024)S(1)}, bf16[4096,768]{0,1:T(8,128)(2,1)}) fusion(bf16[4096,2304]{1,0:T(8,128)(2,1)} %get-tuple-element.20, bf16[1,2304,768]{2,1,0:T(8,128)(2,1)} %all-gather.17.cloned.1.call-done, bf16[1,4096,768]{1,2,0:T(8,128)(2,1)} %copy.10), kind=kOutput, calls=%fused_computation.40 | convolution fusion | flops 14511239168 | bytes 35012608 | tf_op jit(solution)/shard_map/dot_general | solution.py:10
  144.6 8.5 %all-gather.21.cloned.1.call-done = bf16[1,2304,768]{2,1,0:T(8,128)(2,1)} async-done(((bf16[1,288,768]{2,1,0:T(8,128)(2,1)}), bf16[1,2304,768]{2,1,0:T(8,128)(2,1)}) %all-gather.21.cloned.1.call-update) | async-done | bytes 3538960 | tf_op jit(solution)/shard_map/all_gather | solution.py:28
  153.1 21.7 %convolution_convert_fusion.1 = bf16[4096,2304]{1,0:T(8,128)(2,1)} fusion(bf16[1,4096,768]{2,1,0:T(8,128)(2,1)} %param.6, bf16[1,2304,768]{2,1,0:T(8,128)(2,1)} %all-gather.21.cloned.1.call-done), kind=kOutput, calls=%fused_computation.21 | convolution fusion | flops 14504951808 | bytes 28704768 | tf_op jit(solution)/shard_map/transpose(jvp())/dot_general | solution.py:10
  174.8 14.2 %all-gather.23.cloned.1.call-done = bf16[1,768,2304]{2,1,0:T(8,128)(2,1)} async-done(((bf16[1,96,2304]{2,1,0:T(8,128)(2,1)}), bf16[1,768,2304]{2,1,0:T(8,128)(2,1)}) %all-gather.23.cloned.1.call-update) | async-done | bytes 3538960 | tf_op jit(solution)/shard_map/all_gather | solution.py:28
  188.9 23.6 %fusion.37 = f32[4096,2304]{1,0:T(8,128)} fusion(bf16[4096,768]{0,1:T(8,128)(2,1)} %get-tuple-element.23, f32[4096]{0:T(1024)S(1)} %fusion.59, bf16[1,768,2304]{2,1,0:T(8,128)(2,1)} %all-gather.23.cloned.1.call-done), kind=kOutput, calls=%fused_computation.62 | convolution fusion | flops 14504951808 | bytes 47595520 | tf_op jit(solution)/shard_map/jvp()/dot_general | solution.py:22
  212.5 12.3 %all-gather.19.cloned.1.call-done = bf16[1,768,2304]{2,1,0:T(8,128)(2,1)} async-done(((bf16[1,96,2304]{2,1,0:T(8,128)(2,1)}), bf16[1,768,2304]{2,1,0:T(8,128)(2,1)}) %all-gather.19.cloned.1.call-update) | async-done | bytes 3538960 | tf_op jit(solution)/shard_map/all_gather | solution.py:28
  224.9 51.5 %fusion.1 = (bf16[4096,2304]{1,0:T(8,128)(2,1)}, f32[4096,2304]{1,0:T(8,128)}) fusion(f32[4096,2304]{1,0:T(8,128)} %fusion.37, bf16[4096,2304]{1,0:T(8,128)(2,1)} %convolution_convert_fusion.1, bf16[1,768,2304]{2,1,0:T(8,128)(2,1)} %all-gather.19.cloned.1.call-done, bf16[4096,768]{0,1:T(8,128)(2,1)} %get-tuple-element.23, f32[4096]{0:T(1024)S(1)} %fusion.59), kind=kOutput, calls=%fused_computation.7 | convolution fusion | flops 14618198016 | bytes 123092992 | tf_op jit(solution)/shard_map/jvp()/dot_general | solution.py:21
  276.4 21.6 %convolution_convert_fusion.3 = bf16[4096,768]{0,1:T(8,128)(2,1)} fusion(bf16[4096,2304]{1,0:T(8,128)(2,1)} %get-tuple-element.24, bf16[1,768,2304]{2,1,0:T(8,128)(2,1)} %all-gather.19.cloned.1.call-done), kind=kOutput, calls=%fused_computation.46 | convolution fusion | flops 14495514624 | bytes 28704768 | tf_op jit(solution)/shard_map/transpose(jvp())/dot_general | solution.py:21
  297.9 28.2 %fusion.20 = (f32[4096]{0:T(1024)S(1)}, bf16[4096,768]{0,1:T(8,128)(2,1)}) fusion(bf16[4096,768]{0,1:T(8,128)(2,1)} %get-tuple-element.23, bf16[4096,768]{0,1:T(8,128)(2,1)} %convolution_convert_fusion.3, bf16[1,768,2304]{2,1,0:T(8,128)(2,1)S(1)} %copy-done.11, bf16[4096,2304]{1,0:T(8,128)(2,1)} %convolution_convert_fusion.1, ...), kind=kOutput, calls=%fused_computation.42 | convolution fusion | flops 14571008000 | bytes 79052800 | tf_op jit(solution)/shard_map/transpose(jvp())/dot_general | solution.py:22
  326.2 8.0 %fusion.25 = bf16[4096,768]{0,1:T(8,128)(2,1)S(1)} fusion(bf16[4096,768]{0,1:T(8,128)(2,1)} %get-tuple-element.23, bf16[4096,768]{0,1:T(8,128)(2,1)} %get-tuple-element.27, bf16[1,4096,768]{1,2,0:T(8,128)(2,1)} %copy.9, f32[4096]{0:T(1024)S(1)} %multiply_multiply_fusion.1, f32[4096]{0:T(1024)S(1)} %fusion.59), kind=kLoop, calls=%fused_computation.50 | loop fusion | flops 22020096 | bytes 25198592 | tf_op jit(solution)/shard_map/transpose(jvp())/add_any | solution.py:14
  336.8 19.4 %convolution_convert_fusion.7 = bf16[2304,768]{1,0:T(8,128)(2,1)} fusion(bf16[4096,2304]{1,0:T(8,128)(2,1)} %get-tuple-element.20, bf16[4096,768]{0,1:T(8,128)(2,1)S(1)} %fusion.25), kind=kOutput, calls=%fused_computation.61 | convolution fusion | flops 14497284096 | bytes 28704768 | tf_op jit(solution)/shard_map/transpose(jvp())/dot_general | solution.py:10
  356.3 32.4 %fusion.30 = bf16[2304,768]{1,0:T(8,128)(2,1)} fusion(bf16[1,4096,768]{2,1,0:T(8,128)(2,1)} %param.6, f32[4096,2304]{1,0:T(8,128)} %fusion.37, f32[4096,2304]{1,0:T(8,128)} %get-tuple-element.25), kind=kOutput, calls=%fused_computation.56 | convolution fusion | flops 14553907200 | bytes 85327872 | tf_op jit(solution)/shard_map/transpose(jvp())/dot_general | solution.py:10
  388.8 47.7 %fusion.3 = (bf16[4096,2304]{1,0:T(8,128)(2,1)}, bf16[4096,2304]{1,0:T(8,128)(2,1)}) fusion(f32[4096,2304]{1,0:T(8,128)} %fusion.45, f32[4096,2304]{1,0:T(8,128)} %get-tuple-element.21, bf16[4096,768]{0,1:T(8,128)(2,1)} %copy-done, bf16[1,2304,768]{2,1,0:T(8,128)(2,1)S(1)} %copy-done.10), kind=kOutput, calls=%fused_computation.9 | convolution fusion | flops 14618198016 | bytes 123076608 | tf_op jit(solution)/shard_map/transpose(jvp())/dot_general | solution.py:10
  436.5 28.0 %fusion.33 = bf16[768,2304]{1,0:T(8,128)(2,1)} fusion(bf16[4096,2304]{1,0:T(8,128)(2,1)} %get-tuple-element.29, bf16[1,4096,768]{1,2,0:T(8,128)(2,1)} %copy.10, f32[4096]{0:T(1024)S(1)} %copy-done.4, f32[4096,2304]{1,0:T(8,128)} %fusion.45), kind=kOutput, calls=%fused_computation.57 | convolution fusion | flops 14563344384 | bytes 66469888 | tf_op jit(solution)/shard_map/transpose(jvp())/dot_general | solution.py:22
  464.5 28.2 %fusion.34 = bf16[768,2304]{1,0:T(8,128)(2,1)} fusion(bf16[4096,2304]{1,0:T(8,128)(2,1)} %convolution_convert_fusion.1, bf16[4096,768]{0,1:T(8,128)(2,1)} %get-tuple-element.23, f32[4096]{0:T(1024)S(1)} %copy-done.6, f32[4096,2304]{1,0:T(8,128)} %get-tuple-element.25), kind=kOutput, calls=%fused_computation.58 | convolution fusion | flops 14563344384 | bytes 66469888 | tf_op jit(solution)/shard_map/transpose(jvp())/dot_general | solution.py:22
  492.8 20.8 %convolution_convert_fusion.5 = bf16[768,2304]{1,0:T(8,128)(2,1)} fusion(bf16[4096,2304]{1,0:T(8,128)(2,1)} %get-tuple-element.24, bf16[4096,768]{0,1:T(8,128)(2,1)} %get-tuple-element.23, f32[4096]{0:T(1024)S(1)} %copy-done.6), kind=kOutput, calls=%fused_computation.59 | convolution fusion | flops 14504951808 | bytes 28721152 | tf_op jit(solution)/shard_map/transpose(jvp())/dot_general | solution.py:21
  513.7 20.9 %convolution_convert_fusion.6 = bf16[768,2304]{1,0:T(8,128)(2,1)} fusion(bf16[4096,2304]{1,0:T(8,128)(2,1)} %get-tuple-element.28, bf16[1,4096,768]{1,2,0:T(8,128)(2,1)} %copy.10, f32[4096]{0:T(1024)S(1)} %copy-done.4), kind=kOutput, calls=%fused_computation.60 | convolution fusion | flops 14504951808 | bytes 28721152 | tf_op jit(solution)/shard_map/transpose(jvp())/dot_general | solution.py:21
  534.8 21.8 %convolution_convert_fusion.2 = bf16[4096,768]{0,1:T(8,128)(2,1)} fusion(bf16[4096,2304]{1,0:T(8,128)(2,1)} %get-tuple-element.28, bf16[1,768,2304]{2,1,0:T(8,128)(2,1)} %all-gather.13.cloned.1.call-done), kind=kOutput, calls=%fused_computation.45 | convolution fusion | flops 14495514624 | bytes 28704768 | tf_op jit(solution)/shard_map/transpose(jvp())/dot_general | solution.py:21
  556.6 6.7 reduce-scatter.13.cloned.1.call-done
  563.3 51.2 %reduce-scatter.9.cloned.1.call-done = bf16[96,2304]{1,0:T(8,128)(2,1)} async-done(((bf16[768,2304]{1,0:T(8,128)(2,1)}), bf16[96,2304]{1,0:T(8,128)(2,1)}) %reduce-scatter.9.cloned.1.call-update) | async-done | bytes 442384 | tf_op jit(solution)/shard_map/reduce_scatter | solution.py:31
  614.5 51.0 %reduce-scatter.7.cloned.1.call-done = bf16[96,2304]{1,0:T(8,128)(2,1)} async-done(((bf16[768,2304]{1,0:T(8,128)(2,1)}), bf16[96,2304]{1,0:T(8,128)(2,1)}) %reduce-scatter.7.cloned.1.call-update) | async-done | bytes 442384 | tf_op jit(solution)/shard_map/reduce_scatter | solution.py:31
  665.6 27.9 %fusion.17 = (f32[4096]{0:T(1024)S(1)}, bf16[4096,768]{0,1:T(8,128)(2,1)}) fusion(bf16[1,4096,768]{1,2,0:T(8,128)(2,1)} %copy.10, bf16[4096,768]{0,1:T(8,128)(2,1)} %convolution_convert_fusion.2, bf16[1,768,2304]{2,1,0:T(8,128)(2,1)S(1)} %copy-done.9, bf16[4096,2304]{1,0:T(8,128)(2,1)} %get-tuple-element.29, f32[4096,2304]{1,0:T(8,128)} %fusion.45), kind=kOutput, calls=%fused_computation.39 | convolution fusion | flops 14571008000 | bytes 79052800 | tf_op jit(solution)/shard_map/transpose(jvp())/dot_general | solution.py:22
  693.5 11.1 %fusion.24 = bf16[1,4096,768]{1,2,0:T(8,128)(2,1)} fusion(bf16[4096,768]{0,1:T(8,128)(2,1)} %copy-done, bf16[4096,768]{0,1:T(8,128)(2,1)} %get-tuple-element.31, bf16[1,4096,768]{1,2,0:T(8,128)(2,1)} %copy.10, f32[4096]{0:T(1024)S(1)} %multiply_multiply_fusion, f32[4096]{0:T(1024)S(1)} %copy-done.4), kind=kLoop, calls=%fused_computation.49 | loop fusion | flops 22020096 | bytes 25198592 | tf_op jit(solution)/shard_map/broadcast_in_dim | solution.py:44
  704.6 8.6 %copy.11 = bf16[1,4096,768]{2,1,0:T(8,128)(2,1)} copy(bf16[1,4096,768]{1,2,0:T(8,128)(2,1)} %fusion.24) | data formatting | bytes 12582912
  713.2 59.3 %all-reduce.3.cloned.1.call-done = (bf16[1,96,2304]{2,1,0:T(8,128)(2,1)}, bf16[1,96,2304]{2,1,0:T(8,128)(2,1)}, bf16[1,96,2304]{2,1,0:T(8,128)(2,1)}, bf16[1,96,...) async-done(((bf16[1,96,2304]{2,1,0:T(8,128)(2,1)}, bf16[1,96,2304]{2,1,0:T(8,128)(2,1)}, bf16[1,96,2304]{2,1,0:T(8,128)(2,1)}, ...) | async-done | bytes 2654224 | tf_op jit(solution)/shard_map/psum | solution.py:31
  (63 shorter events, 17.5 us)
Async XLA Ops:
  7.2 39.6 %all-gather.13.cloned.1.call-start = ((), (), s32[]{:S(2)}) async-start(), calls=%async_computation.12 | async-start | bytes 3981312 | tf_op jit(solution)/shard_map/all_gather | solution.py:28
  9.3 72.9 %all-gather.15.cloned.1.call-start = ((), (), s32[]{:S(2)}) async-start(), calls=%async_computation.13 | async-start | bytes 3981312 | tf_op jit(solution)/shard_map/all_gather | solution.py:28
  11.5 108.6 %all-gather.17.cloned.1.call-start = ((), (), s32[]{:S(2)}) async-start(), calls=%async_computation.14 | async-start | bytes 3981312 | tf_op jit(solution)/shard_map/all_gather | solution.py:28
  13.7 139.3 %all-gather.21.cloned.1.call-start = ((), (), s32[]{:S(2)}) async-start(), calls=%async_computation.16 | async-start | bytes 3981312 | tf_op jit(solution)/shard_map/all_gather | solution.py:28
  14.3 174.6 %all-gather.23.cloned.1.call-start = ((), (), s32[]{:S(2)}) async-start(), calls=%async_computation.17 | async-start | bytes 3981312 | tf_op jit(solution)/shard_map/all_gather | solution.py:28
  14.9 209.9 %all-gather.19.cloned.1.call-start = ((), (), s32[]{:S(2)}) async-start(), calls=%async_computation.15 | async-start | bytes 3981312 | tf_op jit(solution)/shard_map/all_gather | solution.py:28
  15.5 541.1 %reduce-scatter.15.cloned.1.call-start = ((), (), s32[]{:S(2)}) async-start(), calls=%async_computation.10 | async-start | bytes 3981312 | tf_op jit(solution)/shard_map/reduce_scatter | solution.py:31
  28.2 0.6 copy-start.1
  28.9 53.4 %copy-start.3 = (f32[4096]{0:T(1024)}, f32[4096]{0:T(1024)S(1)}, u32[]{:S(2)}) copy-start(f32[4096]{0:T(1024)S(1)} %fusion.58) | copy-start | bytes 49156
  144.0 0.6 copy-start.7
  144.6 181.6 %copy-start.5 = (f32[4096]{0:T(1024)}, f32[4096]{0:T(1024)S(1)}, u32[]{:S(2)}) copy-start(f32[4096]{0:T(1024)S(1)} %fusion.59) | copy-start | bytes 49156
  276.3 21.6 %copy-start.11 = (bf16[1,768,2304]{2,1,0:T(8,128)(2,1)S(1)}, bf16[1,768,2304]{2,1,0:T(8,128)(2,1)}, u32[]{:S(2)}) copy-start(bf16[1,768,2304]{2,1,0:T(8,128)(2,1)} %all-gather.23.cloned.1.call-done) | copy-start | bytes 10616836
  297.9 28.2 %copy-start.8 = (f32[4096]{0:T(1024)S(1)}, f32[4096]{0:T(1024)}, u32[]{:S(2)}) copy-start(f32[4096]{0:T(1024)} %copy-done.7) | copy-start | bytes 49156
  334.2 2.6 copy-start
  356.3 32.5 %copy-start.10 = (bf16[1,2304,768]{2,1,0:T(8,128)(2,1)S(1)}, bf16[1,2304,768]{2,1,0:T(8,128)(2,1)}, u32[]{:S(2)}) copy-start(bf16[1,2304,768]{2,1,0:T(8,128)(2,1)} %all-gather.17.cloned.1.call-done) | copy-start | bytes 10616836
  356.3 200.4 %reduce-scatter.17.cloned.1.call-start = ((), (), s32[]{:S(2)}) async-start(), calls=%async_computation.11 | async-start | bytes 3981312 | tf_op jit(solution)/shard_map/reduce_scatter | solution.py:31
  388.7 167.9 %reduce-scatter.11.cloned.1.call-start = ((), (), s32[]{:S(2)}) async-start(), calls=%async_computation.8 | async-start | bytes 3981312 | tf_op jit(solution)/shard_map/reduce_scatter | solution.py:31
  388.8 47.7 %copy-start.4 = (f32[4096]{0:T(1024)S(1)}, f32[4096]{0:T(1024)}, u32[]{:S(2)}) copy-start(f32[4096]{0:T(1024)} %copy-done.3) | copy-start | bytes 49156
  436.5 28.0 %copy-start.6 = (f32[4096]{0:T(1024)S(1)}, f32[4096]{0:T(1024)}, u32[]{:S(2)}) copy-start(f32[4096]{0:T(1024)} %copy-done.5) | copy-start | bytes 49156
  464.5 98.9 %reduce-scatter.13.cloned.1.call-start = ((), (), s32[]{:S(2)}) async-start(), calls=%async_computation.9 | async-start | bytes 3981312 | tf_op jit(solution)/shard_map/reduce_scatter | solution.py:31
  492.8 121.7 %reduce-scatter.9.cloned.1.call-start = ((), (), s32[]{:S(2)}) async-start(), calls=%async_computation.7 | async-start | bytes 3981312 | tf_op jit(solution)/shard_map/reduce_scatter | solution.py:31
  513.7 151.9 %reduce-scatter.7.cloned.1.call-start = ((), (), s32[]{:S(2)}) async-start(), calls=%async_computation.6 | async-start | bytes 3981312 | tf_op jit(solution)/shard_map/reduce_scatter | solution.py:31
  534.7 130.9 %copy-start.9 = (bf16[1,768,2304]{2,1,0:T(8,128)(2,1)S(1)}, bf16[1,768,2304]{2,1,0:T(8,128)(2,1)}, u32[]{:S(2)}) copy-start(bf16[1,768,2304]{2,1,0:T(8,128)(2,1)} %all-gather.15.cloned.1.call-done) | copy-start | bytes 10616836
  534.7 237.8 %all-reduce.3.cloned.1.call-start = ((), (), s32[]{:S(2)}) async-start(), calls=%async_computation.18 | async-start | bytes 5308416 | tf_op jit(solution)/shard_map/psum | solution.py:31
  665.6 27.9 %copy-start.2 = (f32[4096]{0:T(1024)S(1)}, f32[4096]{0:T(1024)}, u32[]{:S(2)}) copy-start(f32[4096]{0:T(1024)} %copy-done.1) | copy-start | bytes 49156
Sparse Core Ops, SparseCore 0:
  10.4 36.3 all-gather.12
  48.7 33.5 all-gather.14
  84.1 33.5 all-gather.16
  119.5 33.5 all-gather.20
  155.4 33.5 all-gather.22
  191.3 33.5 all-gather.18
  356.4 47.6 reduce-scatter.14
  407.6 47.6 reduce-scatter.16
  464.6 47.6 reduce-scatter.10
  515.6 47.6 reduce-scatter.12
  566.8 47.6 reduce-scatter.8
  617.9 47.6 reduce-scatter.6
  668.4 104.0 all-reduce.2
where the time goes:
time: 791 us; the launch traced here: 784 us
  matrix products  479 us (61%)
  waiting for transfers between devices  226 us (29%)
  local copies, waits for them, and re-layouts  36 us (5%)
  other arithmetic  28.2 us (4%)
  between operations  14.5 us (2%)
    dot_general x6, matrix products, layer(): up = jnp.dot(a, w['w_up'], preferred_element_type=jnp.float32)  174 us
    dot_general x6, matrix products, layer(): gate = jnp.dot(a, w['w_gate'], preferred_element_type=jnp.float32)  160 us
    dot_general x5, matrix products, matmul(): jnp.dot(a, w, preferred_element_type=jnp.float32).astype(jnp.bfloat16)  145 us
    reduce_scatter x6, waiting for transfers between devices, summed(): lax.psum_scatter(term, 's', scatter_dimension=0, tiled=True)  109 us
    psum x1, waiting for transfers between devices, summed(): lax.psum(lax.psum_scatter(term, 's', scatter_dimension=0, tiled=True), 'r')  59.3 us
    all_gather x6, waiting for transfers between devices, fetched(): lax.all_gather(w[number], 's', axis=0, tiled=True)  56 us
    unnamed x27, local copies, waits for them, and re-layouts  29.7 us
  transfers between devices with their start and end apart: 13, of which 9 were waited for; matrix products, arithmetic and copies ran while one was open for 51% of the time, Pallas kernels for 0%

commit v1 on v0

v1 whole, which is shorter than its diff:
```python
import functools

import jax
import jax.numpy as jnp
from jax import lax
from jax.experimental import pallas as pl
from jax.experimental.pallas import tpu as pltpu
from jax.sharding import Mesh
from jax.sharding import PartitionSpec as P

BF, F32 = jnp.bfloat16, jnp.float32
TB = 1024
CB = 768
NN, NT, TN = ((1,), (0,)), ((1,), (1,)), ((0,), (0,))


def dot(a, b, dims=NN):
    return lax.dot_general(a, b, (dims, ((), ())), preferred_element_type=F32)


def normed(h):
    wide = h.astype(F32)
    return (wide * lax.rsqrt(jnp.mean(wide**2, -1, keepdims=True) + 1e-6)).astype(BF)


def call(kernel, grid, ins, outs, scratch=(), flops=0, aliases=None, name=None):
    def spec(block, index):
        return pl.BlockSpec(memory_space=pl.ANY) if block is None else pl.BlockSpec(block, index)

    size = sum(a.size * a.dtype.itemsize for a, *_ in ins)
    return pl.pallas_call(
        kernel,
        grid=grid,
        in_specs=[spec(b, i) for _, b, i in ins],
        out_specs=[spec(b, i) for *_, b, i in outs],
        out_shape=[jax.ShapeDtypeStruct(s, d) for s, d, *_ in outs],
        scratch_shapes=list(scratch),
        input_output_aliases=aliases or {},
        cost_estimate=pl.CostEstimate(flops=flops, bytes_accessed=size, transcendentals=0),
        compiler_params=pltpu.CompilerParams(vmem_limit_bytes=62 * 2**20, dimension_semantics=("arbitrary",) * len(grid)),
        name=name,
    )(*[a for a, *_ in ins])


def put_rows(w_ref, out, lanes=slice(None)):
    cores, chips, rows = w_ref.shape[:3]
    for chip in range(chips):
        for core in range(cores):
            out[pl.ds((chip * cores + core) * rows, rows), :] = w_ref[core, chip][:, lanes]


def norm_kernel(x_ref, a_ref):
    a_ref[...] = normed(x_ref[...])


def fwd_kernel(a_ref, wg_ref, wu_ref, gate_ref, up_ref, p_ref, wg, wu):
    @pl.when(pl.program_id(1) == 0)
    def _():
        put_rows(wg_ref, wg)
        put_rows(wu_ref, wu)

    a = a_ref[...]
    gate, up = dot(a, wg[...]), dot(a, wu[...])
    gate_ref[...], up_ref[...] = gate, up
    p_ref[...] = (gate * jax.nn.sigmoid(gate) * up).astype(BF)


def down_kernel(p_ref, x_ref, wd_ref, h_ref, a_ref, wd):
    @pl.when(pl.program_id(0) == 0)
    def _():
        put_rows(wd_ref, wd)

    h = x_ref[...] + dot(p_ref[...], wd[...]).astype(BF)
    h_ref[...] = h
    a_ref[...] = normed(h)


def gates(gate, up, dp):
    sig = jax.nn.sigmoid(gate)
    silu = gate * sig
    return silu, (dp * up * (sig + silu * (1 - sig))).astype(BF), (dp * silu).astype(BF)


def finish(dw_ref, acc, lanes=slice(None)):
    cores, chips, rows = dw_ref.shape[:3]
    for chip in range(chips):
        for core in range(cores):
            dw_ref[core, chip, :, lanes] = acc[pl.ds((chip * cores + core) * rows, rows), :].astype(BF)


def back_kernel(saved, chunk, *refs):
    refs = list(refs)
    a_ref, dh_ref, wd_ref = refs[:3]
    if saved:
        gate_ref, up_ref = refs[3:5]
    else:
        wg_ref, wu_ref = refs[3:5]
    refs = refs[5 + (chunk > 0) * (2 if saved else 3) :]
    dgate_ref, dup_ref, dw_ref = refs[:3]
    p_ref = None if saved else refs[3]
    accg, accu, wd, *rest = refs[3 if saved else 4 :]
    t = pl.program_id(0)

    @pl.when(t == 0)
    def _():
        accg[...] = jnp.zeros_like(accg)
        accu[...] = jnp.zeros_like(accu)
        put_rows(wd_ref, wd)
        if not saved:
            put_rows(wg_ref, rest[0])
            put_rows(wu_ref, rest[1])

    a, dh = a_ref[...], dh_ref[...]
    if saved:
        gate, up = gate_ref[...], up_ref[...]
    else:
        gate, up = dot(a, rest[0][...]), dot(a, rest[1][...])
    dp = dot(dh, wd[chunk * CB : (chunk + 1) * CB, :], NT).astype(BF).astype(F32)
    silu, dgate, dup = gates(gate, up, dp)
    dgate_ref[...], dup_ref[...] = dgate, dup
    if not saved:
        p_ref[...] = (silu * up).astype(BF)
    accg[...] += dot(a, dgate, TN)
    accu[...] += dot(a, dup, TN)

    @pl.when(t == pl.num_programs(0) - 1)
    def _():
        finish(dw_ref, accg, slice(0, CB))
        finish(dw_ref, accu, slice(CB, 2 * CB))


def down_back_kernel(p_ref, dh_ref, dw_ref, acc):
    t = pl.program_id(0)

    @pl.when(t == 0)
    def _():
        acc[...] = jnp.zeros_like(acc)

    acc[...] += dot(p_ref[...], dh_ref[...], TN)

    @pl.when(t == pl.num_programs(0) - 1)
    def _():
        finish(dw_ref, acc)


def input_back_kernel(dgate_ref, dup_ref, h_ref, dh_ref, wg_ref, wu_ref, out_ref, wg, wu):
    @pl.when(pl.program_id(0) == 0)
    def _():
        put_rows(wg_ref, wg)
        put_rows(wu_ref, wu)

    da = dot(dgate_ref[...], wg[...], NT).astype(BF) + dot(dup_ref[...], wu[...], NT).astype(BF)
    g, h = da.astype(F32), h_ref[...].astype(F32)
    scale = lax.rsqrt(jnp.mean(h**2, -1, keepdims=True) + 1e-6)
    dn = g * scale - h * (scale**3 * jnp.mean(g * h, -1, keepdims=True))
    out_ref[...] = dh_ref[...] + dn.astype(BF)


def solution(mesh):
    sizes = mesh.shape
    rep, r, s = sizes["rep"], sizes["r"], sizes["s"]
    chips, cores = s // 2, 2
    fine = Mesh(mesh.devices.reshape(rep, r, chips, cores), ("rep", "r", "chip", "core"))

    def gathered(w):
        return lax.all_gather(lax.all_gather(w, "chip"), "core")

    def scattered(term):
        return lax.psum_scatter(lax.psum_scatter(term, "core"), "chip")

    def step(x, dy, w_gate, w_up, w_down):
        x, dy = x[0], dy[0]
        tokens, d = x.shape
        layers, _, ff = w_gate.shape
        nt, nc = tokens // TB, ff // CB
        row, whole = (lambda t: (t, 0)), (lambda *_: (0, 0, 0, 0))
        rows_d, rows_f = d // s, ff // s
        mm = 2 * tokens * d * ff
        blockrow = (TB, d)
        gu = [gathered(jnp.concatenate([w_gate[l], w_up[l]], 1)) for l in range(layers)]
        wd = [gathered(w_down[l]) for l in range(layers)]
        wd_block = (cores, chips, rows_f, d)
        w_block = (cores, chips, rows_d, CB)
        w_half = (cores, chips, rows_d, ff)

        (a1,) = call(norm_kernel, (nt,), [(x, blockrow, row)], [((tokens, d), BF, blockrow, row)], flops=10**6, name="norm")
        gate, up, p1 = call(
            fwd_kernel,
            (nc, nt),
            [
                (a1, blockrow, lambda c, t: (t, 0)),
                (gu[0], w_block, lambda c, t: (0, 0, 0, c)),
                (gu[0], w_block, lambda c, t: (0, 0, 0, nc + c)),
            ],
            [((tokens, ff), dt, (TB, CB), lambda c, t: (t, c)) for dt in (F32, F32, BF)],
            [pltpu.VMEM((d, CB), BF)] * 2,
            2 * mm,
            name="fwd",
        )
        h1, a2 = call(
            down_kernel,
            (nt,),
            [(p1, (TB, ff), row), (x, blockrow, row), (wd[0], wd_block, whole)],
            [((tokens, d), BF, blockrow, row)] * 2,
            [pltpu.VMEM((ff, d), BF)],
            mm,
            name="down",
        )

        def back(l, a, dh, h, saved):
            scratch = [pltpu.VMEM((d, CB), F32)] * 2 + [pltpu.VMEM((ff, d), BF)]
            so_far, dgu = [], []
            for c in range(nc):
                ins = [(a, blockrow, row), (dh, blockrow, row), (wd[l], wd_block, whole)]
                here = lambda t, c=c: (t, c)
                if saved:
                    ins += [(gate, (TB, CB), here), (up, (TB, CB), here)]
                else:
                    ins += [(gu[l], w_block, lambda t, c=c: (0, 0, 0, c)), (gu[l], w_block, lambda t, c=c: (0, 0, 0, nc + c))]
                outs = [((tokens, ff), BF, (TB, CB), here)] * 2 + [((cores, chips, rows_d, 2 * CB), BF, (cores, chips, rows_d, 2 * CB), whole)]
                if not saved:
                    outs += [outs[0]]
                aliases = {}
                if c:
                    for i, buffer in enumerate(so_far):
                        aliases[len(ins)] = i if i < 2 else 3
                        ins.append((buffer, None, None))
                got = call(
                    functools.partial(back_kernel, saved, c),
                    (nt,),
                    ins,
                    outs,
                    scratch + ([] if saved else [pltpu.VMEM((d, CB), BF)] * 2),
                    (3 if saved else 5) * mm // nc,
                    aliases,
                    f"back{l}_{c}",
                )
                so_far = got[:2] + got[3:]
                dgu.append(got[2])
            dgate, dup = so_far[:2]
            p = p1 if saved else so_far[2]
            return dgate, dup, p, dgu

        def down_back(p, dh):
            return call(
                down_back_kernel,
                (nt,),
                [(p, (TB, ff), row), (dh, blockrow, row)],
                [((cores, chips, rows_f, d), BF, (cores, chips, rows_f, d), whole)],
                [pltpu.VMEM((ff, d), F32)],
                mm,
                name="down_back",
            )[0]

        def input_back(l, dgate, dup, h, dh):
            return call(
                input_back_kernel,
                (nt,),
                [
                    (dgate, (TB, ff), row),
                    (dup, (TB, ff), row),
                    (h, blockrow, row),
                    (dh, blockrow, row),
                    (gu[l], w_half, lambda t: (0, 0, 0, 0)),
                    (gu[l], w_half, lambda t: (0, 0, 0, 1)),
                ],
                [((tokens, d), BF, blockrow, row)],
                [pltpu.VMEM((d, ff), BF)] * 2,
                2 * mm,
                name="input_back",
            )[0]

        dgate, dup, p2, dgu2 = back(1, a2, dy, h1, False)
        dwd2 = down_back(p2, dy)
        dh1 = input_back(1, dgate, dup, h1, dy)
        mine2 = [scattered(t) for t in dgu2] + [scattered(dwd2)]
        mine2 = [lax.psum(t, "r") for t in mine2]
        dwd1 = down_back(p1, dh1)
        dgate, dup, _, dgu1 = back(0, a1, dh1, x, True)
        mine1 = [scattered(dwd1)] + [scattered(t) for t in dgu1]
        mine2, mine1 = lax.optimization_barrier((mine2, mine1))
        mine1 = [lax.psum(t, "r") for t in mine1]
        dx = input_back(0, dgate, dup, x, dh1)

        g = jnp.stack([jnp.concatenate([t[:, :CB] for t in m], 1) for m in (mine1[1:], mine2[:nc])])
        u = jnp.stack([jnp.concatenate([t[:, CB:] for t in m], 1) for m in (mine1[1:], mine2[:nc])])
        return dx[None], g, u, jnp.stack([mine1[0], mine2[nc]])

    states, cut = P(("rep", "r", "chip", "core"), None, None), P(None, ("chip", "core"), None)
    return jax.shard_map(
        step,
        mesh=fine,
        in_specs=(states, states) + (cut,) * 3,
        out_specs=(states,) + (P("rep", ("chip", "core"), None),) * 3,
        check_vma=False,
    )
```

time: 791 us -> 964 us (1.22)
  matrix products: 479 us -> 0 us
  Pallas kernels: 0 us -> 386 us
  waiting for transfers between devices: 226 us -> 539 us
  local copies, waits for them, and re-layouts: 36 us -> 8.67 us
  other arithmetic: 28.2 us -> 5.03 us
    dot_general x17 -> x0, matrix products: 479 us -> none  [the longest x6 174 us: layer(): up = jnp.dot(a, w['w_up'], preferred_element_type=jnp.float32)]
    pallas_call x0 -> x13, Pallas kernels: none -> 386 us  [call(): pl.pallas_call(kernel, grid=grid, in_specs=[spec(b, i) for _, b, i in ins...]
    unnamed x13 -> x34, waiting for transfers between devices: 1.74 us -> 225 us
    all_gather x6 -> x8, waiting for transfers between devices: 56 us -> 179 us  [gathered(): return lax.all_gather(lax.all_gather(w, 'chip'), 'core')]
    reduce_scatter x6 -> x8, waiting for transfers between devices: 109 us -> 11.2 us  [scattered(): return lax.psum_scatter(lax.psum_scatter(term, 'core'), 'chip')]
    psum x1 -> x2, waiting for transfers between devices: 59.3 us -> 124 us  [the longest x1 64 us: step(): mine2 = [lax.psum(t, 'r') for t in mine2]]
    unnamed x27 -> x6, local copies, waits for them, and re-layouts: 29.7 us -> 0.01 us
    broadcast_in_dim x1 -> x0, other arithmetic: 11.1 us -> none  [step(): by_h[None]]
  transfers between devices with their start and end apart: 13 -> 26, of which waited for: 9 -> 15; matrix products, arithmetic and copies ran while one was open for 51% -> 1% of each run, Pallas kernels for 0% -> 37%
where the time goes in v1:
time: 964 us; the launch traced here: 955 us
  waiting for transfers between devices  539 us (56%)
  Pallas kernels  386 us (40%)
  between operations  14.7 us (2%)
    pallas_call x13, Pallas kernels, call(): pl.pallas_call(kernel, grid=grid, in_specs=[spec(b, i) for _, b, i in ins...  386 us
    unnamed x34, waiting for transfers between devices  225 us
    all_gather x8, waiting for transfers between devices, gathered(): return lax.all_gather(lax.all_gather(w, 'chip'), 'core')  179 us
    psum x1, waiting for transfers between devices, step(): mine2 = [lax.psum(t, 'r') for t in mine2]  64 us
    psum x1, waiting for transfers between devices, step(): mine1 = [lax.psum(t, 'r') for t in mine1]  60 us
  transfers between devices with their start and end apart: 26, of which 15 were waited for; matrix products, arithmetic and copies ran while one was open for 1% of the time, Pallas kernels for 37%

profile of v1, /device:TPU:0, one launch (start us, length us, event | category | flops | bytes accessed | tf_op | source)
XLA Modules:
  0.0 954.6 jit_solution(16613453934596360478)
XLA Ops:
  7.2 1.6 slice_bitcast_fusion
  12.7 47.3 %all-gather.19.cloned.1.call-done = bf16[384,4608]{1,0:T(8,128)(2,1)} async-done(((bf16[96,4608]{1,0:T(8,128)(2,1)}), bf16[384,4608]{1,0:T(8,128)(2,1)}) %all-gather.19.cloned.1.call-update) | async-done | bytes 3538960 | tf_op jit(solution)/shard_map/all_gather | solution.py:166
  60.1 34.6 %all-gather.15.cloned.1.call-done = bf16[4,288,768]{2,1,0:T(8,128)(2,1)} async-done(((bf16[1,288,768]{2,1,0:T(8,128)(2,1)}), bf16[4,288,768]{2,1,0:T(8,128)(2,1)}) %all-gather.15.cloned.1.call-update) | async-done | bytes 1769488 | tf_op jit(solution)/shard_map/all_gather | solution.py:166
  94.7 34.6 %all-gather.17.cloned.1.call-done = bf16[4,288,768]{2,1,0:T(8,128)(2,1)} async-done(((bf16[1,288,768]{2,1,0:T(8,128)(2,1)}), bf16[4,288,768]{2,1,0:T(8,128)(2,1)}) %all-gather.17.cloned.1.call-update) | async-done | bytes 1769488 | tf_op jit(solution)/shard_map/all_gather | solution.py:166
  129.3 49.0 %all-gather.27.cloned.1.call-done = bf16[384,4608]{1,0:T(8,128)(2,1)} async-done(((bf16[96,4608]{1,0:T(8,128)(2,1)}), bf16[384,4608]{1,0:T(8,128)(2,1)}) %all-gather.27.cloned.1.call-update) | async-done | bytes 3538960 | tf_op jit(solution)/shard_map/all_gather | solution.py:166
  178.4 6.6 norm.1.a_ref.refs_0_
  185.1 13.4 %all-gather.21.cloned.1.call-done = bf16[8,96,4608]{2,1,0:T(8,128)(2,1)} async-done(((bf16[4,96,4608]{2,1,0:T(8,128)(2,1)}), bf16[8,96,4608]{2,1,0:T(8,128)(2,1)}) %all-gather.21.cloned.1.call-update) | async-done | bytes 7077904 | tf_op jit(solution)/shard_map/all_gather | solution.py:166
  198.5 44.0 %fwd.1 = (f32[4096,2304]{1,0:T(8,128)}, f32[4096,2304]{1,0:T(8,128)}, bf16[4096,2304]{1,0:T(8,128)(2,1)}) custom-call(bf16[4096,768]{1,0:T(8,128)(2,1)} %norm.1.a_ref.refs_0_, bf16[2,4,96,4608]{3,2,1,0:T(8,128)(2,1)} %bitcast.69, bf16[2,4,96,4608]{3,2,1,0:T(8,128)(2,1)} %bitcast.70), custom_call_target="tpu_custom_call" | custom-call | flops 28991029248 | bytes 20447232 | tf_op jit(solution)/shard_map/fwd/pallas_call | solution.py:31
  242.5 22.2 %down.1 = (bf16[4096,768]{1,0:T(8,128)(2,1)}, bf16[4096,768]{1,0:T(8,128)(2,1)}) custom-call(bf16[4096,2304]{1,0:T(8,128)(2,1)} %get-tuple-element.38.p_ref, bf16[4096,768]{1,0:T(8,128)(2,1)} %bitcast.49, bf16[2,4,288,768]{3,2,1,0:T(8,128)(2,1)} %bitcast.44), custom_call_target="tpu_custom_call" | custom-call | flops 14495514624 | bytes 28704768 | tf_op jit(solution)/shard_map/down/pallas_call | solution.py:31
  264.7 35.4 %back1_0.1 = (bf16[4096,2304]{1,0:T(8,128)(2,1)}, bf16[4096,2304]{1,0:T(8,128)(2,1)}, bf16[2,4,96,1536]{3,2,1,0:T(8,128)(2,1)}, bf16[4096,2304]{1,0:T(8,128)(2,1)}) custom-call(bf16[4096,768]{1,0:T(8,128)(2,1)} %get-tuple-element.39.refs_0_, bf16[4096,768]{1,0:T(8,128)(2,1)} %bitcast.81, bf16[2,4,288,768]{3,2,1,0:T(8,128)(2,1)} %bitcast.86, ...), custom_call_target="tpu_custom_call" | custom-call | flops 24159191040 | bytes 30277632 | tf_op jit(solution)/shard_map/back1_0/pallas_call | solution.py:31
  300.5 35.4 %back1_1.1 = (bf16[4096,2304]{1,0:T(8,128)(2,1)}, bf16[4096,2304]{1,0:T(8,128)(2,1)}, bf16[2,4,96,1536]{3,2,1,0:T(8,128)(2,1)}, bf16[4096,2304]{1,0:T(8,128)(2,1)}) custom-call(bf16[4096,768]{1,0:T(8,128)(2,1)} %get-tuple-element.39.refs_0_, bf16[4096,768]{1,0:T(8,128)(2,1)} %bitcast.82, ...), custom_call_target="tpu_custom_call", output_to_operand_aliasing={{0}: (5, {}), {1}: (6, {}), {3}: (7, {})} | custom-call | flops 24159191040 | bytes 86900736 | tf_op jit(solution)/shard_map/back1_1/pallas_call | solution.py:31
  335.9 35.4 %back1_2.1 = (bf16[4096,2304]{1,0:T(8,128)(2,1)}, bf16[4096,2304]{1,0:T(8,128)(2,1)}, bf16[2,4,96,1536]{3,2,1,0:T(8,128)(2,1)}, bf16[4096,2304]{1,0:T(8,128)(2,1)}) custom-call(bf16[4096,768]{1,0:T(8,128)(2,1)} %get-tuple-element.39.refs_0_, bf16[4096,768]{1,0:T(8,128)(2,1)} %bitcast.83, ...), custom_call_target="tpu_custom_call", output_to_operand_aliasing={{0}: (5, {}), {1}: (6, {}), {3}: (7, {})} | custom-call | flops 24159191040 | bytes 86900736 | tf_op jit(solution)/shard_map/back1_2/pallas_call | solution.py:31
  372.1 21.2 %down_back.2 = bf16[2,4,288,768]{3,2,1,0:T(8,128)(2,1)} custom-call(bf16[4096,2304]{1,0:T(8,128)(2,1)} %get-tuple-element.60.p_ref, bf16[4096,768]{1,0:T(8,128)(2,1)} %bitcast.84), custom_call_target="tpu_custom_call" | custom-call | flops 14495514624 | bytes 25165824 | tf_op jit(solution)/shard_map/down_back/pallas_call | solution.py:31
  393.4 42.5 %input_back.2.refs_1_.dh_ref = bf16[4096,768]{1,0:T(8,128)(2,1)} custom-call(bf16[4096,2304]{1,0:T(8,128)(2,1)} %get-tuple-element.46.dgate_ref, bf16[4096,2304]{1,0:T(8,128)(2,1)} %get-tuple-element.47.dup_ref, bf16[4096,768]{1,0:T(8,128)(2,1)} %get-tuple-element.48.h_ref, bf16[4096,768]{1,0:T(8,128)(2,1)} %bitcast.85, bf16[2,4,96,4608]{3,2,1,0:T(8,128)(2,1)} %bitcast.79, ...), custom_call_target="tpu_custom_call" | custom-call | flops 28991029248 | bytes 64487424 | tf_op jit(solution)/shard_map/input_back/pallas_call | solution.py:31
  435.9 26.4 %back0_0.1 = (bf16[4096,2304]{1,0:T(8,128)(2,1)}, bf16[4096,2304]{1,0:T(8,128)(2,1)}, bf16[2,4,96,1536]{3,2,1,0:T(8,128)(2,1)}) custom-call(bf16[4096,768]{1,0:T(8,128)(2,1)} %norm.1.a_ref.refs_0_, bf16[4096,768]{1,0:T(8,128)(2,1)} %input_back.2.refs_1_.dh_ref, bf16[2,4,288,768]{3,2,1,0:T(8,128)(2,1)} %bitcast.45, f32[4096,2304]{1,0:T(8,128)} %get-tuple-element.49.refs_3_, ...), custom_call_target="tpu_custom_call" | custom-call | flops 14495514624 | bytes 91619328 | tf_op jit(solution)/shard_map/back0_0/pallas_call | solution.py:31
  462.4 26.4 %back0_1.1 = (bf16[4096,2304]{1,0:T(8,128)(2,1)}, bf16[4096,2304]{1,0:T(8,128)(2,1)}, bf16[2,4,96,1536]{3,2,1,0:T(8,128)(2,1)}) custom-call(bf16[4096,768]{1,0:T(8,128)(2,1)} %norm.1.a_ref.refs_0_, bf16[4096,768]{1,0:T(8,128)(2,1)} %input_back.2.refs_1_.dh_ref, bf16[2,4,288,768]{3,2,1,0:T(8,128)(2,1)} %bitcast.46, ...), custom_call_target="tpu_custom_call", output_to_operand_aliasing={{0}: (5, {}), {1}: (6, {})} | custom-call | flops 14495514624 | bytes 129368064 | tf_op jit(solution)/shard_map/back0_1/pallas_call | solution.py:31
  488.8 26.4 %back0_2.1 = (bf16[4096,2304]{1,0:T(8,128)(2,1)}, bf16[4096,2304]{1,0:T(8,128)(2,1)}, bf16[2,4,96,1536]{3,2,1,0:T(8,128)(2,1)}) custom-call(bf16[4096,768]{1,0:T(8,128)(2,1)} %norm.1.a_ref.refs_0_, bf16[4096,768]{1,0:T(8,128)(2,1)} %input_back.2.refs_1_.dh_ref, bf16[2,4,288,768]{3,2,1,0:T(8,128)(2,1)} %bitcast.47, ...), custom_call_target="tpu_custom_call", output_to_operand_aliasing={{0}: (5, {}), {1}: (6, {})} | custom-call | flops 14495514624 | bytes 129368064 | tf_op jit(solution)/shard_map/back0_2/pallas_call | solution.py:31
  515.9 21.5 %down_back.3 = bf16[2,4,288,768]{3,2,1,0:T(8,128)(2,1)} custom-call(bf16[4096,2304]{1,0:T(8,128)(2,1)} %get-tuple-element.38.p_ref, bf16[4096,768]{1,0:T(8,128)(2,1)} %input_back.2.refs_1_.dh_ref), custom_call_target="tpu_custom_call" | custom-call | flops 14495514624 | bytes 25165824 | tf_op jit(solution)/shard_map/down_back/pallas_call | solution.py:31
  542.1 11.1 %reduce-scatter.41.cloned.1.call-done = bf16[1,4,288,768]{3,2,1,0:T(8,128)(2,1)} async-done(((bf16[2,4,288,768]{3,2,1,0:T(8,128)(2,1)}), bf16[1,4,288,768]{3,2,1,0:T(8,128)(2,1)}) %reduce-scatter.41.cloned.1.call-update) | async-done | bytes 1769488 | tf_op jit(solution)/shard_map/reduce_scatter | solution.py:169
  553.3 32.6 %reduce-scatter.49.cloned.1.call-done = bf16[1,96,1536]{2,1,0:T(8,128)(2,1)} async-done(((bf16[4,96,1536]{2,1,0:T(8,128)(2,1)}), bf16[1,96,1536]{2,1,0:T(8,128)(2,1)}) %reduce-scatter.49.cloned.1.call-update) | async-done | bytes 294928
  585.8 31.5 %reduce-scatter.53.cloned.1.call-done = bf16[1,96,1536]{2,1,0:T(8,128)(2,1)} async-done(((bf16[4,96,1536]{2,1,0:T(8,128)(2,1)}), bf16[1,96,1536]{2,1,0:T(8,128)(2,1)}) %reduce-scatter.53.cloned.1.call-update) | async-done | bytes 294928
  617.4 31.7 %reduce-scatter.51.cloned.1.call-done = bf16[1,96,1536]{2,1,0:T(8,128)(2,1)} async-done(((bf16[4,96,1536]{2,1,0:T(8,128)(2,1)}), bf16[1,96,1536]{2,1,0:T(8,128)(2,1)}) %reduce-scatter.51.cloned.1.call-update) | async-done | bytes 294928
  649.0 35.2 %reduce-scatter.55.cloned.1.call-done = bf16[1,288,768]{2,1,0:T(8,128)(2,1)} async-done(((bf16[4,288,768]{2,1,0:T(8,128)(2,1)}), bf16[1,288,768]{2,1,0:T(8,128)(2,1)}) %reduce-scatter.55.cloned.1.call-update) | async-done | bytes 442384
  684.3 42.4 %input_back.3 = bf16[4096,768]{1,0:T(8,128)(2,1)} custom-call(bf16[4096,2304]{1,0:T(8,128)(2,1)} %get-tuple-element.55.dgate_ref, bf16[4096,2304]{1,0:T(8,128)(2,1)} %get-tuple-element.56.dup_ref, bf16[4096,768]{1,0:T(8,128)(2,1)} %bitcast.50, bf16[4096,768]{1,0:T(8,128)(2,1)} %input_back.2.refs_1_.dh_ref, bf16[2,4,96,4608]{3,2,1,0:T(8,128)(2,1)} %bitcast.71, ...), custom_call_target="tpu_custom_call" | custom-call | flops 28991029248 | bytes 64487424 | tf_op jit(solution)/shard_map/input_back/pallas_call | solution.py:31
  726.7 20.9 %reduce-scatter.63.cloned.1.call-done = bf16[1,96,1536]{2,1,0:T(8,128)(2,1)} async-done(((bf16[4,96,1536]{2,1,0:T(8,128)(2,1)}), bf16[1,96,1536]{2,1,0:T(8,128)(2,1)}) %reduce-scatter.63.cloned.1.call-update) | async-done | bytes 294928
  747.6 31.7 %reduce-scatter.61.cloned.1.call-done = bf16[1,96,1536]{2,1,0:T(8,128)(2,1)} async-done(((bf16[4,96,1536]{2,1,0:T(8,128)(2,1)}), bf16[1,96,1536]{2,1,0:T(8,128)(2,1)}) %reduce-scatter.61.cloned.1.call-update) | async-done | bytes 294928
  779.2 35.2 %reduce-scatter.57.cloned.1.call-done = bf16[1,288,768]{2,1,0:T(8,128)(2,1)} async-done(((bf16[4,288,768]{2,1,0:T(8,128)(2,1)}), bf16[1,288,768]{2,1,0:T(8,128)(2,1)}) %reduce-scatter.57.cloned.1.call-update) | async-done | bytes 442384
  814.4 64.0 %all-reduce.15.cloned.1.call-done = (bf16[96,1536]{1,0:T(8,128)(2,1)}, bf16[96,1536]{1,0:T(8,128)(2,1)}, bf16[96,1536]{1,0:T(8,128)(2,1)}, bf16[288,768]{1,0:T(8,128)(2,1)}) async-done(((bf16[96,1536]{1,0:T(8,128)(2,1)}, bf16[96,1536]{1,0:T(8,128)(2,1)}, bf16[96,1536]{1,0:T(8,128)(2,1)}, bf16[288,768]{1,0:T(8,128)(2,1)}), (bf16[96,1536]{1,0:T(8,128)(2,1)}, bf16[96,1536]{1,0:T(8,128)(2,1)}, ...) | async-done | bytes 1327120 | tf_op jit(solution)/shard_map/psum | solution.py:277
  878.4 1.0 fusion.4
  880.5 1.0 fusion.6
  881.5 60.0 %all-reduce.13.cloned.1.call-done = (bf16[96,1536]{1,0:T(8,128)(2,1)}, bf16[96,1536]{1,0:T(8,128)(2,1)}, bf16[96,1536]{1,0:T(8,128)(2,1)}, bf16[1,288,768]{2,1,0:T(8,128)(2,1)}) async-done(((bf16[96,1536]{1,0:T(8,128)(2,1)}, bf16[96,1536]{1,0:T(8,128)(2,1)}, bf16[96,1536]{1,0:T(8,128)(2,1)}, bf16[1,288,768]{2,1,0:T(8,128)(2,1)}), (bf16[96,1536]{1,0:T(8,128)(2,1)}, bf16[96,1536]{1,0:T(8,128)(2,1)}, ...) | async-done | bytes 1327120 | tf_op jit(solution)/shard_map/psum | solution.py:282
  941.5 1.1 fusion.3
  (82 shorter events, 16.8 us)
Async XLA Ops:
  7.2 2.7 copy-start
  7.2 52.8 %all-gather.19.cloned.1.call-start = ((), (), s32[]{:S(2)}) async-start(), calls=%async_computation.26 | async-start | bytes 4423680 | tf_op jit(solution)/shard_map/all_gather | solution.py:166
  9.8 84.8 %all-gather.15.cloned.1.call-start = ((), (), s32[]{:S(2)}) async-start(), calls=%async_computation.16 | async-start | bytes 2211840 | tf_op jit(solution)/shard_map/all_gather | solution.py:166
  10.9 118.4 %all-gather.17.cloned.1.call-start = ((), (), s32[]{:S(2)}) async-start(), calls=%async_computation.17 | async-start | bytes 2211840 | tf_op jit(solution)/shard_map/all_gather | solution.py:166
  11.6 166.8 %all-gather.27.cloned.1.call-start = ((), (), s32[]{:S(2)}) async-start(), calls=%async_computation.30 | async-start | bytes 4423680 | tf_op jit(solution)/shard_map/all_gather | solution.py:166
  12.6 185.8 %all-gather.21.cloned.1.call-start = ((), (), s32[]{:S(2)}) async-start(), calls=%async_computation.27 | async-start | bytes 10616832 | tf_op jit(solution)/shard_map/all_gather | solution.py:166
  60.0 182.5 %all-gather.23.cloned.1.call-start = ((), (), s32[]{:S(2)}) async-start(), calls=%async_computation.28 | async-start | bytes 5308416 | tf_op jit(solution)/shard_map/all_gather | solution.py:166
  94.6 170.0 %all-gather.25.cloned.1.call-start = ((), (), s32[]{:S(2)}) async-start(), calls=%async_computation.29 | async-start | bytes 5308416 | tf_op jit(solution)/shard_map/all_gather | solution.py:166
  129.3 135.4 %all-gather.29.cloned.1.call-start = ((), (), s32[]{:S(2)}) async-start(), calls=%async_computation.31 | async-start | bytes 10616832 | tf_op jit(solution)/shard_map/all_gather | solution.py:166
  178.4 359.0 %reduce-scatter.33.cloned.1.call-start = ((), (), s32[]{:S(2)}) async-start(), calls=%async_computation.18 | async-start | bytes 3538944 | tf_op jit(solution)/shard_map/reduce_scatter | solution.py:169
  300.1 237.9 %reduce-scatter.37.cloned.1.call-start = ((), (), s32[]{:S(2)}) async-start(), calls=%async_computation.20 | async-start | bytes 3538944 | tf_op jit(solution)/shard_map/reduce_scatter | solution.py:169
  371.3 167.3 %reduce-scatter.35.cloned.1.call-start = ((), (), s32[]{:S(2)}) async-start(), calls=%async_computation.19 | async-start | bytes 3538944 | tf_op jit(solution)/shard_map/reduce_scatter | solution.py:169
  372.1 167.3 %reduce-scatter.39.cloned.1.call-start = ((), (), s32[]{:S(2)}) async-start(), calls=%async_computation.21 | async-start | bytes 5308416 | tf_op jit(solution)/shard_map/reduce_scatter | solution.py:169
  393.3 146.6 %reduce-scatter.43.cloned.1.call-start = ((), (), s32[]{:S(2)}) async-start(), calls=%async_computation.23 | async-start | bytes 3538944 | tf_op jit(solution)/shard_map/reduce_scatter | solution.py:169
  462.3 78.4 %reduce-scatter.47.cloned.1.call-start = ((), (), s32[]{:S(2)}) async-start(), calls=%async_computation.25 | async-start | bytes 3538944 | tf_op jit(solution)/shard_map/reduce_scatter | solution.py:169
  515.2 26.2 %reduce-scatter.45.cloned.1.call-start = ((), (), s32[]{:S(2)}) async-start(), calls=%async_computation.24 | async-start | bytes 3538944 | tf_op jit(solution)/shard_map/reduce_scatter | solution.py:169
  515.8 37.4 %reduce-scatter.41.cloned.1.call-start = ((), (), s32[]{:S(2)}) async-start(), calls=%async_computation.22 | async-start | bytes 5308416 | tf_op jit(solution)/shard_map/reduce_scatter | solution.py:169
  537.4 48.5 %reduce-scatter.49.cloned.1.call-start = ((), (), s32[]{:S(2)}) async-start(), calls=%async_computation.32 | async-start | bytes 1474560
  538.0 79.4 %reduce-scatter.53.cloned.1.call-start = ((), (), s32[]{:S(2)}) async-start(), calls=%async_computation.34 | async-start | bytes 1474560
  538.5 110.5 %reduce-scatter.51.cloned.1.call-start = ((), (), s32[]{:S(2)}) async-start(), calls=%async_computation.33 | async-start | bytes 1474560
  539.3 144.9 %reduce-scatter.55.cloned.1.call-start = ((), (), s32[]{:S(2)}) async-start(), calls=%async_computation.35 | async-start | bytes 2211840
  539.9 186.8 %reduce-scatter.59.cloned.1.call-start = ((), (), s32[]{:S(2)}) async-start(), calls=%async_computation.37 | async-start | bytes 1474560
  540.6 206.9 %reduce-scatter.63.cloned.1.call-start = ((), (), s32[]{:S(2)}) async-start(), calls=%async_computation.39 | async-start | bytes 1474560
  541.4 237.9 %reduce-scatter.61.cloned.1.call-start = ((), (), s32[]{:S(2)}) async-start(), calls=%async_computation.38 | async-start | bytes 1474560
  542.1 272.3 %reduce-scatter.57.cloned.1.call-start = ((), (), s32[]{:S(2)}) async-start(), calls=%async_computation.36 | async-start | bytes 2211840
  553.2 325.2 %all-reduce.15.cloned.1.call-start = ((), (), s32[]{:S(2)}) async-start(), calls=%async_computation.41 | async-start | bytes 2654208 | tf_op jit(solution)/shard_map/psum | solution.py:277
  684.2 257.3 %all-reduce.13.cloned.1.call-start = ((), (), s32[]{:S(2)}) async-start(), calls=%async_computation.40 | async-start | bytes 2654208 | tf_op jit(solution)/shard_map/psum | solution.py:282
  941.5 5.2 copy-start.1
  941.5 5.2 copy-start.2
Sparse Core Ops, SparseCore 0:
  10.4 49.5 all-gather.18
  62.4 32.1 all-gather.14
  97.0 32.1 all-gather.16
  131.5 46.7 all-gather.26
  179.8 18.6 all-gather.20
  199.9 14.1 all-gather.22
  215.6 14.1 all-gather.24
  231.2 19.8 all-gather.28
  300.2 10.6 reduce-scatter.32
  371.5 10.6 reduce-scatter.36
  384.4 10.6 reduce-scatter.34
  397.2 11.6 reduce-scatter.38
  462.4 10.6 reduce-scatter.42
  515.4 10.6 reduce-scatter.46
  528.2 10.6 reduce-scatter.44
  541.5 11.6 reduce-scatter.40
  556.0 29.8 reduce-scatter.48
  588.6 28.7 reduce-scatter.52
  620.3 28.7 reduce-scatter.50
  651.9 32.2 reduce-scatter.54
  687.1 28.7 reduce-scatter.58
  718.8 28.7 reduce-scatter.62
  750.5 28.7 reduce-scatter.60
  782.1 32.2 reduce-scatter.56
  817.0 61.3 all-reduce.14
  880.9 60.5 all-reduce.12
